TPU v7x, 32 devices: a whole 2x2x4 slice. The times are simulated.
32 devices in a mesh: bank: 8 (over z, core), zero: 4 (over y, x).
Axes of the slice: x: 2, y: 2, z: 4, core: 2. Of those that a mesh axis runs over, the one named last changes fastest.
Arguments:
- master_gate: float32 [64, 2048, 1408], P('bank', 'zero'), may hold values from -0.1875 to 0.1875
- master_up: float32 [64, 2048, 1408], P('bank', 'zero'), may hold values from -0.1875 to 0.1875
- master_down: float32 [64, 1408, 2048], P('bank', None, 'zero'), may hold values from -0.21875 to 0.21875
- router_weight: float32 [2048, 64], P('zero', 'bank'), may hold values from -0.125 to 0.125
- router_gain: float32 [2048], P('zero'), may hold values from 0.25 to 1.75
Outputs:
- final_gate: bfloat16 [64, 2048, 1408], P('bank', None, 'zero')
- final_up: bfloat16 [64, 2048, 1408], P('bank', None, 'zero')
- final_down: bfloat16 [64, 1408, 2048], P('bank', 'zero')
- scale_gate: float32 [64, 1408], P('bank', 'zero')
- scale_up: float32 [64, 1408], P('bank', 'zero')
- scale_down: float32 [64, 1408], P('bank', 'zero')
- serve_router: bfloat16 [2048, 64], replicated
All inputs are finite; a program needn't handle non-finite values. Where the computation divides by a largest or mean magnitude, that divisor is 1e-20 or more.
Results may differ from a plain program's by a relative error of at most 0.0013.
Values may be sent and summed in bfloat16 or wider, within the bound.
A program may use at most 192 MiB of HBM per device.

v0:
```python
import jax
import jax.numpy as jnp
from jax import lax
from jax.sharding import PartitionSpec as P

D_MODEL = 2048


def local(master_gate, master_up, master_down, router_weight, router_gain):
    total_gate, total_up, total_down = lax.psum(
        (
            jnp.sum(jnp.abs(master_gate), axis=1),
            jnp.sum(jnp.abs(master_up), axis=1),
            jnp.sum(jnp.abs(master_down), axis=2),
        ),
        "zero",
    )
    scale_gate = total_gate / D_MODEL
    scale_up = total_up / D_MODEL
    scale_down = total_down / D_MODEL
    narrow_gate, narrow_up, narrow_down = (
        (master_gate / jnp.expand_dims(scale_gate, 1)).astype(jnp.bfloat16),
        (master_up / jnp.expand_dims(scale_up, 1)).astype(jnp.bfloat16),
        (master_down / jnp.expand_dims(scale_down, 2)).astype(jnp.bfloat16),
    )
    final_gate, final_up = (
        lax.all_to_all(narrow_gate, "zero", split_axis=2, concat_axis=1, tiled=True),
        lax.all_to_all(narrow_up, "zero", split_axis=2, concat_axis=1, tiled=True),
    )
    final_down = lax.all_to_all(narrow_down, "zero", split_axis=1, concat_axis=2, tiled=True)
    scale_gate = lax.dynamic_slice_in_dim(
        scale_gate, lax.axis_index("zero") * final_gate.shape[2], final_gate.shape[2], axis=1
    )
    scale_up = lax.dynamic_slice_in_dim(
        scale_up, lax.axis_index("zero") * final_up.shape[2], final_up.shape[2], axis=1
    )
    scale_down = lax.dynamic_slice_in_dim(
        scale_down, lax.axis_index("zero") * final_down.shape[1], final_down.shape[1], axis=1
    )
    part_router = (router_weight * router_gain[:, None]).astype(jnp.bfloat16)
    row_router = lax.all_gather(part_router, "zero", axis=0, tiled=True)
    serve_router = lax.all_gather(row_router, "bank", axis=1, tiled=True)
    return (final_gate, final_up, final_down, scale_gate, scale_up, scale_down, serve_router)


def solution(mesh):
    placed = (
        P("bank", "zero", None),
        P("bank", "zero", None),
        P("bank", None, "zero"),
        P("zero", "bank"),
        P("zero"),
    )
    return jax.shard_map(
        local,
        mesh=mesh,
        in_specs=placed,
        out_specs=(
            P("bank", None, "zero"),
            P("bank", None, "zero"),
            P("bank", "zero", None),
            P("bank", "zero"),
            P("bank", "zero"),
            P("bank", "zero"),
            P(),
        ),
        check_vma=False,
    )
```

profile of v0, /device:TPU:0, one launch (start us, length us, event | category | flops | bytes accessed | tf_op | source)
XLA Modules:
  0.0 620.0 jit_solution(9753489696694195745)
XLA Ops:
  7.2 0.0 all-reduce.3.cloned.1.call-start
  7.2 0.0 copy-start
  7.2 9.0 %abs_reduce_fusion = f32[8,1408]{1,0:T(8,128)} fusion(f32[8,1408,512]{2,1,0:T(8,128)} %param.7), kind=kLoop, calls=%fused_computation.2 | loop fusion | flops 11523072 | bytes 23113728 | tf_op jit(solution)/shard_map/reduce_sum | solution.py:14
  16.2 5.2 copy-done
  21.4 10.8 %abs_reduce_fusion.1 = (f32[8,1408]{1,0:T(8,128)}, f32[8,1408]{1,0:T(8,128)}) fusion(f32[8,512,1408]{2,1,0:T(8,128)S(1)} %copy-done, f32[8,512,1408]{2,1,0:T(8,128)} %param.5), kind=kLoop, calls=%fused_computation.4 | loop fusion | flops 23046144 | bytes 46227456 | tf_op jit(solution)/shard_map/reduce_sum | solution.py:13
  32.2 0.0 all-reduce.3.cloned.1.call-update
  32.2 23.7 %copy.28 = f32[8,512,1408]{1,0,2:T(8,128)} copy(f32[8,512,1408]{2,1,0:T(8,128)} %param.6) | data formatting | bytes 46137344 | tf_op args[1]
  55.9 21.4 %all-reduce.3.cloned.1.call-done = (f32[8,1408]{1,0:T(8,128)}, f32[8,1408]{1,0:T(8,128)}, f32[8,1408]{1,0:T(8,128)}) async-done(((f32[8,1408]{1,0:T(8,128)}, f32[8,1408]{1,0:T(8,128)}, f32[8,1408]{1,0:T(8,128)}), (f32[8,1408]{1,0:T(8,128)}, f32[8,1408]{1,0:T(8,128)}, f32[8,1408]{1,0:T(8,128)})) %all-reduce.3.cloned.1.call-update) | async-done | bytes 135184 | tf_op jit(solution)/shard_map/psum | solution.py:10
  77.3 0.8 broadcast_multiply_fusion.1
  78.1 0.3 copy.27
  78.4 13.3 %divide_convert_fusion = bf16[8,512,1408]{1,0,2:T(8,128)(2,1)} fusion(f32[8,512,1408]{1,0,2:T(8,128)} %copy.28, f32[8,1408]{0,1:T(8,128)S(1)} %copy.27), kind=kLoop, calls=%fused_computation.3 | loop fusion | flops 11534336 | bytes 34648064 | tf_op jit(solution)/shard_map/convert_element_type | solution.py:23
  91.7 6.2 %all-to-all-start.1 = ((bf16[8,512,1408]{1,0,2:T(8,128)(2,1)}), bf16[8,512,1408]{1,0,2:T(8,128)(2,1)}, u32[]{:S(2)}, u32[]{:S(2)}) async-start(bf16[8,512,1408]{1,0,2:T(8,128)(2,1)} %divide_convert_fusion), calls=%async_computation.1 | async-start | bytes 23068672 | tf_op jit(solution)/shard_map/all_to_all | solution.py:28
  97.9 0.0 copy-start.2
  98.0 23.7 %copy.24 = f32[8,512,1408]{1,0,2:T(8,128)} copy(f32[8,512,1408]{2,1,0:T(8,128)} %param.5) | data formatting | bytes 46137344 | tf_op args[0]
  121.6 0.0 copy-done.2
  121.6 0.3 copy.23
  121.9 0.0 copy-start.1
  121.9 13.3 %divide_convert_fusion.1 = bf16[8,512,1408]{1,0,2:T(8,128)(2,1)} fusion(f32[8,512,1408]{1,0,2:T(8,128)} %copy.24, f32[8,1408]{0,1:T(8,128)S(1)} %copy.23), kind=kLoop, calls=%fused_computation.5 | loop fusion | flops 11534336 | bytes 34648064 | tf_op jit(solution)/shard_map/convert_element_type | solution.py:22
  135.2 88.5 %all-to-all-done.1 = bf16[8,512,1408]{1,0,2:T(8,128)(2,1)} async-done(((bf16[8,512,1408]{1,0,2:T(8,128)(2,1)}), bf16[8,512,1408]{1,0,2:T(8,128)(2,1)}, u32[]{:S(2)}, u32[]{:S(2)}) %all-to-all-start.1) | async-done | bytes 11534368 | tf_op jit(solution)/shard_map/all_to_all | solution.py:28
  223.7 6.2 all-to-all-start
  229.9 0.0 copy-done.1
  229.9 0.3 copy.31
  230.2 0.0 copy-start.3
  230.2 0.0 copy-start.4
  230.2 29.5 %fusion = bf16[8,1408,512]{2,0,1:T(8,128)(2,1)} fusion(f32[8,1408,512]{2,1,0:T(8,128)} %param.7, f32[8,1408]{0,1:T(8,128)S(1)} %copy.31), kind=kLoop, calls=%fused_computation.1 | loop fusion | flops 11534336 | bytes 34648064 | tf_op jit(solution)/shard_map/convert_element_type | solution.py:24
  259.7 95.7 %all-to-all-done = bf16[8,512,1408]{1,0,2:T(8,128)(2,1)} async-done(((bf16[8,512,1408]{1,0,2:T(8,128)(2,1)}), bf16[8,512,1408]{1,0,2:T(8,128)(2,1)}, u32[]{:S(2)}, u32[]{:S(2)}) %all-to-all-start) | async-done | bytes 11534368 | tf_op jit(solution)/shard_map/all_to_all | solution.py:27
  355.4 6.2 %all-to-all-start.2 = ((bf16[8,1408,512]{2,0,1:T(8,128)(2,1)}), bf16[8,1408,512]{2,0,1:T(8,128)(2,1)}, u32[]{:S(2)}, u32[]{:S(2)}) async-start(bf16[8,1408,512]{2,0,1:T(8,128)(2,1)} %fusion), calls=%async_computation.2 | async-start | bytes 23068672 | tf_op jit(solution)/shard_map/all_to_all | solution.py:30
  361.7 0.0 copy-done.3
  361.7 0.0 copy-done.4
  361.7 128.8 %all_gather.6 = bf16[2048,8]{0,1:T(8,128)(2,1)S(1)} all-gather(bf16[512,8]{0,1:T(8,128)(2,1)S(1)} %multiply_convert_fusion), channel_id=1, replica_groups=mesh['bank'=8,'zero'=4] {'zero'}, dimensions={0}, use_global_device_ids=true | all-gather | bytes 40960 | tf_op jit(solution)/shard_map/all_gather | solution.py:41
  490.6 14.4 %all_gather.7 = bf16[2048,64]{0,1:T(8,128)(2,1)S(1)} all-gather(bf16[2048,8]{0,1:T(8,128)(2,1)S(1)} %all_gather.6), channel_id=1, replica_groups=mesh['bank'=8,'zero'=4] {'bank'}, dimensions={1}, use_global_device_ids=true | all-gather | bytes 294912 | tf_op jit(solution)/shard_map/all_gather | solution.py:42
  505.0 0.7 constant_dynamic-slice_fusion
  505.6 0.7 constant_dynamic-slice_fusion.1
  506.3 0.7 constant_dynamic-slice_fusion.2
  507.0 15.9 %copy.30 = bf16[8,4,512,352]{2,1,3,0:T(4,128)(2,1)} copy(bf16[8,4,512,352]{2,0,3,1:T(8,128)(2,1)} %bitcast.5) | data formatting | bytes 23068672 | tf_op jit(solution)/shard_map/all_to_all | solution.py:28
  522.9 19.3 %all_to_all.46 = bf16[8,2048,352]{1,2,0:T(8,128)(2,1)} reshape(bf16[8,4,512,352]{2,1,3,0:T(4,128)(2,1)} %copy.30) | data formatting | bytes 23068672 | tf_op jit(solution)/shard_map/all_to_all | solution.py:28
  542.1 15.9 %copy.26 = bf16[8,4,512,352]{2,1,3,0:T(4,128)(2,1)} copy(bf16[8,4,512,352]{2,0,3,1:T(8,128)(2,1)} %bitcast.2) | data formatting | bytes 23068672 | tf_op jit(solution)/shard_map/all_to_all | solution.py:27
  558.0 19.3 %all_to_all.42 = bf16[8,2048,352]{1,2,0:T(8,128)(2,1)} reshape(bf16[8,4,512,352]{2,1,3,0:T(4,128)(2,1)} %copy.26) | data formatting | bytes 23068672 | tf_op jit(solution)/shard_map/all_to_all | solution.py:27
  577.3 0.0 all-to-all-done.2
  577.3 15.9 %copy.33 = bf16[8,352,4,512]{3,2,1,0:T(4,128)(2,1)} copy(bf16[8,352,4,512]{3,0,1,2:T(8,128)(2,1)} %bitcast.7) | data formatting | bytes 23068672 | tf_op jit(solution)/shard_map/all_to_all | solution.py:30
  593.2 19.3 %all_to_all.50 = bf16[8,352,2048]{2,1,0:T(8,128)(2,1)} reshape(bf16[8,352,4,512]{3,2,1,0:T(4,128)(2,1)} %copy.33) | data formatting | bytes 23068672 | tf_op jit(solution)/shard_map/all_to_all | solution.py:30
  612.5 0.7 copy.43
  (3 shorter events, 0.0 us)
Async XLA Ops:
  7.2 70.2 %all-reduce.3.cloned.1.call-start = ((), (), s32[]{:S(2)}) async-start(), calls=%async_computation.3 | async-start | bytes 270336 | tf_op jit(solution)/shard_map/psum | solution.py:10
  7.2 14.2 %copy-start = (f32[8,512,1408]{2,1,0:T(8,128)S(1)}, f32[8,512,1408]{2,1,0:T(8,128)}, u32[]{:S(2)}) copy-start(f32[8,512,1408]{2,1,0:T(8,128)} %param.6) | copy-start | bytes 69206016
  91.7 132.0 %all-to-all-start.1 = ((bf16[8,512,1408]{1,0,2:T(8,128)(2,1)}), bf16[8,512,1408]{1,0,2:T(8,128)(2,1)}, u32[]{:S(2)}, u32[]{:S(2)}) async-start(bf16[8,512,1408]{1,0,2:T(8,128)(2,1)} %divide_convert_fusion), calls=%async_computation.1 | async-start | bytes 23068672 | tf_op jit(solution)/shard_map/all_to_all | solution.py:28
  97.9 23.7 %copy-start.2 = (f32[8,1408]{1,0:T(8,128)S(1)}, f32[8,1408]{1,0:T(8,128)}, u32[]{:S(2)}) copy-start(f32[8,1408]{1,0:T(8,128)} %get-tuple-element.7) | copy-start | bytes 135172
  121.9 108.0 %copy-start.1 = (f32[8,1408]{1,0:T(8,128)S(1)}, f32[8,1408]{1,0:T(8,128)}, u32[]{:S(2)}) copy-start(f32[8,1408]{1,0:T(8,128)} %get-tuple-element.9) | copy-start | bytes 135172
  223.7 131.7 %all-to-all-start = ((bf16[8,512,1408]{1,0,2:T(8,128)(2,1)}), bf16[8,512,1408]{1,0,2:T(8,128)(2,1)}, u32[]{:S(2)}, u32[]{:S(2)}) async-start(bf16[8,512,1408]{1,0,2:T(8,128)(2,1)} %divide_convert_fusion.1), calls=%async_computation | async-start | bytes 23068672 | tf_op jit(solution)/shard_map/all_to_all | solution.py:27
  230.2 131.5 %copy-start.3 = (f32[512,8]{0,1:T(8,128)S(1)}, f32[512,8]{0,1:T(8,128)}, u32[]{:S(2)}) copy-start(f32[512,8]{0,1:T(8,128)} %param.8) | copy-start | bytes 49156
  230.2 131.5 %copy-start.4 = (f32[512]{0:T(512)S(1)}, f32[512]{0:T(512)}, u32[]{:S(2)}) copy-start(f32[512]{0:T(512)} %param.9) | copy-start | bytes 6148
  355.4 221.8 %all-to-all-start.2 = ((bf16[8,1408,512]{2,0,1:T(8,128)(2,1)}), bf16[8,1408,512]{2,0,1:T(8,128)(2,1)}, u32[]{:S(2)}, u32[]{:S(2)}) async-start(bf16[8,1408,512]{2,0,1:T(8,128)(2,1)} %fusion), calls=%async_computation.2 | async-start | bytes 23068672 | tf_op jit(solution)/shard_map/all_to_all | solution.py:30
Sparse Core Ops, SparseCore 0:
  32.3 44.9 all-reduce.2
where the time goes:
time: 623 us; the launch traced here: 620 us
  waiting for transfers between devices  206 us (33%)
  local copies, waits for them, and re-layouts  162 us (26%)
  blocking collectives  143 us (23%)
  other arithmetic  76.7 us (12%)
  starting transfers between devices  18.6 us (3%)
  between operations  14.2 us (2%)
    all_gather x1, blocking collectives, local(): row_router = lax.all_gather(part_router, 'zero', axis=0, tiled=True)  129 us
    all_to_all x1, waiting for transfers between devices, local(): lax.all_to_all(narrow_gate, 'zero', split_axis=2, concat_axis=1, tiled=True)  95.7 us
    all_to_all x1, waiting for transfers between devices, local(): lax.all_to_all(narrow_up, 'zero', split_axis=2, concat_axis=1, tiled=True)  88.5 us
    unnamed x13, local copies, waits for them, and re-layouts  53.3 us
    all_to_all x2, local copies, waits for them, and re-layouts, local(): lax.all_to_all(narrow_down, 'zero', split_axis=1, concat_axis=2, tiled=True)  35.2 us
    all_to_all x2, local copies, waits for them, and re-layouts, local(): lax.all_to_all(narrow_up, 'zero', split_axis=2, concat_axis=1, tiled=True)  35.1 us
    all_to_all x2, local copies, waits for them, and re-layouts, local(): lax.all_to_all(narrow_gate, 'zero', split_axis=2, concat_axis=1, tiled=True)  35.1 us
    convert_element_type x1, other arithmetic, local(): (master_down / jnp.expand_dims(scale_down, 2)).astype(jnp.bfloat16)  29.5 us
  transfers between devices with their start and end apart: 4, of which 3 were waited for; matrix products, arithmetic and copies ran while one was open for 20% of the time, Pallas kernels for 0%

commit v1 on v0

--- a/solution.py
+++ b/solution.py
@@ -7,6 +7,15 @@
 
 
 def local(master_gate, master_up, master_down, router_weight, router_gain):
+
+    def _open_chunk(mine_x, peer_axis):
+        return jnp.concatenate(
+            lax.all_to_all(
+                jnp.stack(jnp.split(mine_x, lax.axis_size(peer_axis), 1)), peer_axis, 0, 0
+            ),
+            axis=2,
+        )
+
     total_gate, total_up, total_down = lax.psum(
         (
             jnp.sum(jnp.abs(master_gate), axis=1),
@@ -27,7 +36,7 @@
         lax.all_to_all(narrow_gate, "zero", split_axis=2, concat_axis=1, tiled=True),
         lax.all_to_all(narrow_up, "zero", split_axis=2, concat_axis=1, tiled=True),
     )
-    final_down = lax.all_to_all(narrow_down, "zero", split_axis=1, concat_axis=2, tiled=True)
+    final_down = _open_chunk(narrow_down, "zero")
     scale_gate = lax.dynamic_slice_in_dim(
         scale_gate, lax.axis_index("zero") * final_gate.shape[2], final_gate.shape[2], axis=1
     )

time: 623 us -> 597 us (0.958)
  local copies, waits for them, and re-layouts: 162 us -> 138 us
  other arithmetic: 76.7 us -> 62.1 us
  waiting for transfers between devices: 206 us -> 220 us
    all_to_all x2 -> x0, local copies, waits for them, and re-layouts: 35.2 us -> none  [local(): lax.all_to_all(narrow_down, 'zero', split_axis=1, concat_axis=2, tiled=True)]
    all_to_all x1, waiting for transfers between devices: 88.5 us -> 110 us  [local(): lax.all_to_all(narrow_up, 'zero', split_axis=2, concat_axis=1, tiled=True)]
    convert_element_type x1, other arithmetic: 29.5 us -> 9.46 us  [local(): (master_down / jnp.expand_dims(scale_down, 2)).astype(jnp.bfloat16)]
    reshape x0 -> x1, local copies, waits for them, and re-layouts: none -> 10.2 us  [_open_chunk(): jnp.concatenate(lax.all_to_all(jnp.stack(jnp.split(mine_x, lax.axis_size(...]
    all_to_all x1, waiting for transfers between devices: 95.7 us -> 88.5 us  [local(): lax.all_to_all(narrow_gate, 'zero', split_axis=2, concat_axis=1, tiled=True)]
  transfers between devices with their start and end apart: 4 -> 4, of which waited for: 3 -> 3; matrix products, arithmetic and copies ran while one was open for 20% -> 19% of each run, Pallas kernels for 0% -> 0%
where the time goes in v1:
time: 597 us; the launch traced here: 595 us
  waiting for transfers between devices  220 us (37%)
  blocking collectives  143 us (24%)
  local copies, waits for them, and re-layouts  138 us (23%)
  other arithmetic  62.1 us (10%)
  starting transfers between devices  18.6 us (3%)
  between operations  14.2 us (2%)
    all_gather x1, blocking collectives, local(): row_router = lax.all_gather(part_router, 'zero', axis=0, tiled=True)  129 us
    all_to_all x1, waiting for transfers between devices, local(): lax.all_to_all(narrow_up, 'zero', split_axis=2, concat_axis=1, tiled=True)  110 us
    all_to_all x1, waiting for transfers between devices, local(): lax.all_to_all(narrow_gate, 'zero', split_axis=2, concat_axis=1, tiled=True)  88.5 us
    unnamed x13, local copies, waits for them, and re-layouts  53.3 us
    all_to_all x2, local copies, waits for them, and re-layouts, local(): lax.all_to_all(narrow_gate, 'zero', split_axis=2, concat_axis=1, tiled=True)  35.1 us
    all_to_all x2, local copies, waits for them, and re-layouts, local(): lax.all_to_all(narrow_up, 'zero', split_axis=2, concat_axis=1, tiled=True)  35.1 us
    psum x1, waiting for transfers between devices, local(): lax.psum((jnp.sum(jnp.abs(master_gate), axis=1), jnp.sum(jnp.abs(master_u...  21.4 us
    all_gather x1, blocking collectives, local(): serve_router = lax.all_gather(row_router, 'bank', axis=1, tiled=True)  14.2 us
  transfers between devices with their start and end apart: 4, of which 3 were waited for; matrix products, arithmetic and copies ran while one was open for 19% of the time, Pallas kernels for 0%

profile of v1, /device:TPU:0, one launch (start us, length us, event | category | flops | bytes accessed | tf_op | source)
XLA Modules:
  0.0 595.0 jit_solution(5036282671248505699)
XLA Ops:
  7.2 0.0 all-reduce.3.cloned.1.call-start
  7.2 0.0 copy-start
  7.2 9.0 %abs_reduce_fusion = f32[8,1408]{1,0:T(8,128)} fusion(f32[8,1408,512]{2,1,0:T(8,128)} %param.7), kind=kLoop, calls=%fused_computation.1 | loop fusion | flops 11523072 | bytes 23113728 | tf_op jit(solution)/shard_map/reduce_sum | solution.py:23
  16.2 5.2 copy-done
  21.4 10.9 %abs_reduce_fusion.1 = (f32[8,1408]{1,0:T(8,128)}, f32[8,1408]{1,0:T(8,128)}) fusion(f32[8,512,1408]{2,1,0:T(8,128)} %param.6, f32[8,512,1408]{2,1,0:T(8,128)S(1)} %copy-done), kind=kLoop, calls=%fused_computation.3 | loop fusion | flops 23046144 | bytes 46227456 | tf_op jit(solution)/shard_map/reduce_sum | solution.py:22
  32.3 0.0 all-reduce.3.cloned.1.call-update
  32.4 23.7 %copy.24 = f32[8,512,1408]{1,0,2:T(8,128)} copy(f32[8,512,1408]{2,1,0:T(8,128)} %param.5) | data formatting | bytes 46137344 | tf_op args[0]
  56.0 21.4 %all-reduce.3.cloned.1.call-done = (f32[8,1408]{1,0:T(8,128)}, f32[8,1408]{1,0:T(8,128)}, f32[8,1408]{1,0:T(8,128)}) async-done(((f32[8,1408]{1,0:T(8,128)}, f32[8,1408]{1,0:T(8,128)}, f32[8,1408]{1,0:T(8,128)}), (f32[8,1408]{1,0:T(8,128)}, f32[8,1408]{1,0:T(8,128)}, f32[8,1408]{1,0:T(8,128)})) %all-reduce.3.cloned.1.call-update) | async-done | bytes 135184 | tf_op jit(solution)/shard_map/psum | solution.py:19
  77.5 0.8 broadcast_multiply_fusion.2
  78.3 0.3 copy.23
  78.5 13.3 %divide_convert_fusion.2 = bf16[8,512,1408]{1,0,2:T(8,128)(2,1)} fusion(f32[8,512,1408]{1,0,2:T(8,128)} %copy.24, f32[8,1408]{0,1:T(8,128)S(1)} %copy.23), kind=kLoop, calls=%fused_computation.4 | loop fusion | flops 11534336 | bytes 34648064 | tf_op jit(solution)/shard_map/convert_element_type | solution.py:31
  91.9 6.2 %all-to-all-start = ((bf16[8,512,1408]{1,0,2:T(8,128)(2,1)}), bf16[8,512,1408]{1,0,2:T(8,128)(2,1)}, u32[]{:S(2)}, u32[]{:S(2)}) async-start(bf16[8,512,1408]{1,0,2:T(8,128)(2,1)} %divide_convert_fusion.2), calls=%async_computation | async-start | bytes 23068672 | tf_op jit(solution)/shard_map/all_to_all | solution.py:36
  98.1 0.0 copy-start.2
  98.1 23.7 %copy.28 = f32[8,512,1408]{1,0,2:T(8,128)} copy(f32[8,512,1408]{2,1,0:T(8,128)} %param.6) | data formatting | bytes 46137344 | tf_op args[1]
  121.7 0.0 copy-done.2
  121.8 0.3 copy.27
  122.0 13.3 %divide_convert_fusion.1 = bf16[8,512,1408]{1,0,2:T(8,128)(2,1)} fusion(f32[8,512,1408]{1,0,2:T(8,128)} %copy.28, f32[8,1408]{0,1:T(8,128)S(1)} %copy.27), kind=kLoop, calls=%fused_computation.2 | loop fusion | flops 11534336 | bytes 34648064 | tf_op jit(solution)/shard_map/convert_element_type | solution.py:32
  135.3 0.0 copy-start.1
  135.3 88.5 %all-to-all-done = bf16[8,512,1408]{1,0,2:T(8,128)(2,1)} async-done(((bf16[8,512,1408]{1,0,2:T(8,128)(2,1)}), bf16[8,512,1408]{1,0,2:T(8,128)(2,1)}, u32[]{:S(2)}, u32[]{:S(2)}) %all-to-all-start) | async-done | bytes 11534368 | tf_op jit(solution)/shard_map/all_to_all | solution.py:36
  223.9 6.2 %all-to-all-start.1 = ((bf16[8,512,1408]{1,0,2:T(8,128)(2,1)}), bf16[8,512,1408]{1,0,2:T(8,128)(2,1)}, u32[]{:S(2)}, u32[]{:S(2)}) async-start(bf16[8,512,1408]{1,0,2:T(8,128)(2,1)} %divide_convert_fusion.1), calls=%async_computation.1 | async-start | bytes 23068672 | tf_op jit(solution)/shard_map/all_to_all | solution.py:37
  230.0 0.0 copy-done.1
  230.0 9.5 %divide_convert_fusion = bf16[8,1408,512]{2,1,0:T(8,128)(2,1)S(1)} fusion(f32[8,1408,512]{2,1,0:T(8,128)} %param.7, f32[8,1408]{1,0:T(8,128)S(1)} %broadcast_multiply_fusion), kind=kLoop, calls=%fused_computation | loop fusion | flops 11534336 | bytes 34648064 | tf_op jit(solution)/shard_map/convert_element_type | solution.py:33
  239.5 1.1 slice_bitcast_fusion.3
  240.7 5.3 pad_maximum_fusion
  246.0 0.0 copy-start.3
  246.0 0.0 copy-start.4
  246.0 109.6 %all-to-all-done.1 = bf16[8,512,1408]{1,0,2:T(8,128)(2,1)} async-done(((bf16[8,512,1408]{1,0,2:T(8,128)(2,1)}), bf16[8,512,1408]{1,0,2:T(8,128)(2,1)}, u32[]{:S(2)}, u32[]{:S(2)}) %all-to-all-start.1) | async-done | bytes 11534368 | tf_op jit(solution)/shard_map/all_to_all | solution.py:37
  355.6 6.2 %all-to-all-start.2 = ((bf16[4,8,352,512]{3,2,1,0:T(8,128)(2,1)}), bf16[4,8,352,512]{3,2,1,0:T(8,128)(2,1)}, u32[]{:S(2)}, u32[]{:S(2)}) async-start(bf16[4,8,352,512]{3,2,1,0:T(8,128)(2,1)} %pad_maximum_fusion), calls=%async_computation.2 | async-start | bytes 23068672 | tf_op jit(solution)/shard_map/all_to_all | solution.py:13
  361.8 0.0 copy-done.3
  361.8 0.0 copy-done.4
  361.9 128.8 %all_gather.6 = bf16[2048,8]{0,1:T(8,128)(2,1)S(1)} all-gather(bf16[512,8]{0,1:T(8,128)(2,1)S(1)} %multiply_convert_fusion), channel_id=1, replica_groups=mesh['bank'=8,'zero'=4] {'zero'}, dimensions={0}, use_global_device_ids=true | all-gather | bytes 40960 | tf_op jit(solution)/shard_map/all_gather | solution.py:50
  490.7 14.2 %all_gather.7 = bf16[2048,64]{0,1:T(8,128)(2,1)S(1)} all-gather(bf16[2048,8]{0,1:T(8,128)(2,1)S(1)} %all_gather.6), channel_id=1, replica_groups=mesh['bank'=8,'zero'=4] {'bank'}, dimensions={1}, use_global_device_ids=true | all-gather | bytes 294912 | tf_op jit(solution)/shard_map/all_gather | solution.py:51
  504.9 0.7 constant_dynamic-slice_fusion.2
  505.6 0.7 constant_dynamic-slice_fusion.1
  506.3 0.7 constant_dynamic-slice_fusion
  506.9 15.9 %copy.26 = bf16[8,4,512,352]{2,1,3,0:T(4,128)(2,1)} copy(bf16[8,4,512,352]{2,0,3,1:T(8,128)(2,1)} %bitcast.2) | data formatting | bytes 23068672 | tf_op jit(solution)/shard_map/all_to_all | solution.py:36
  522.8 19.3 %all_to_all.32 = bf16[8,2048,352]{1,2,0:T(8,128)(2,1)} reshape(bf16[8,4,512,352]{2,1,3,0:T(4,128)(2,1)} %copy.26) | data formatting | bytes 23068672 | tf_op jit(solution)/shard_map/all_to_all | solution.py:36
  542.1 15.9 %copy.30 = bf16[8,4,512,352]{2,1,3,0:T(4,128)(2,1)} copy(bf16[8,4,512,352]{2,0,3,1:T(8,128)(2,1)} %bitcast.5) | data formatting | bytes 23068672 | tf_op jit(solution)/shard_map/all_to_all | solution.py:37
  558.0 19.3 %all_to_all.36 = bf16[8,2048,352]{1,2,0:T(8,128)(2,1)} reshape(bf16[8,4,512,352]{2,1,3,0:T(4,128)(2,1)} %copy.30) | data formatting | bytes 23068672 | tf_op jit(solution)/shard_map/all_to_all | solution.py:37
  577.2 0.0 all-to-all-done.2
  577.2 10.2 %copy.34 = bf16[4,8,44,8,512]{4,3,0,2,1:T(8,128)(2,1)} copy(bf16[4,8,44,8,512]{4,3,2,1,0:T(8,128)(2,1)} %bitcast.11) | data formatting | bytes 23068672 | tf_op jit(solution)/shard_map/reshape | solution.py:12
  587.5 0.7 copy.39
  (3 shorter events, 0.0 us)
Async XLA Ops:
  7.2 70.3 %all-reduce.3.cloned.1.call-start = ((), (), s32[]{:S(2)}) async-start(), calls=%async_computation.3 | async-start | bytes 270336 | tf_op jit(solution)/shard_map/psum | solution.py:19
  7.2 14.2 %copy-start = (f32[8,512,1408]{2,1,0:T(8,128)S(1)}, f32[8,512,1408]{2,1,0:T(8,128)}, u32[]{:S(2)}) copy-start(f32[8,512,1408]{2,1,0:T(8,128)} %param.5) | copy-start | bytes 69206016
  91.9 132.0 %all-to-all-start = ((bf16[8,512,1408]{1,0,2:T(8,128)(2,1)}), bf16[8,512,1408]{1,0,2:T(8,128)(2,1)}, u32[]{:S(2)}, u32[]{:S(2)}) async-start(bf16[8,512,1408]{1,0,2:T(8,128)(2,1)} %divide_convert_fusion.2), calls=%async_computation | async-start | bytes 23068672 | tf_op jit(solution)/shard_map/all_to_all | solution.py:36
  98.1 23.7 %copy-start.2 = (f32[8,1408]{1,0:T(8,128)S(1)}, f32[8,1408]{1,0:T(8,128)}, u32[]{:S(2)}) copy-start(f32[8,1408]{1,0:T(8,128)} %get-tuple-element.8) | copy-start | bytes 135172
  135.3 94.7 %copy-start.1 = (f32[8,1408]{1,0:T(8,128)S(1)}, f32[8,1408]{1,0:T(8,128)}, u32[]{:S(2)}) copy-start(f32[8,1408]{1,0:T(8,128)} %get-tuple-element.9) | copy-start | bytes 135172
  223.9 131.7 %all-to-all-start.1 = ((bf16[8,512,1408]{1,0,2:T(8,128)(2,1)}), bf16[8,512,1408]{1,0,2:T(8,128)(2,1)}, u32[]{:S(2)}, u32[]{:S(2)}) async-start(bf16[8,512,1408]{1,0,2:T(8,128)(2,1)} %divide_convert_fusion.1), calls=%async_computation.1 | async-start | bytes 23068672 | tf_op jit(solution)/shard_map/all_to_all | solution.py:37
  246.0 115.8 %copy-start.3 = (f32[512,8]{0,1:T(8,128)S(1)}, f32[512,8]{0,1:T(8,128)}, u32[]{:S(2)}) copy-start(f32[512,8]{0,1:T(8,128)} %param.8) | copy-start | bytes 49156
  246.0 115.9 %copy-start.4 = (f32[512]{0:T(512)S(1)}, f32[512]{0:T(512)}, u32[]{:S(2)}) copy-start(f32[512]{0:T(512)} %param.9) | copy-start | bytes 6148
  355.6 221.7 %all-to-all-start.2 = ((bf16[4,8,352,512]{3,2,1,0:T(8,128)(2,1)}), bf16[4,8,352,512]{3,2,1,0:T(8,128)(2,1)}, u32[]{:S(2)}, u32[]{:S(2)}) async-start(bf16[4,8,352,512]{3,2,1,0:T(8,128)(2,1)} %pad_maximum_fusion), calls=%async_computation.2 | async-start | bytes 23068672 | tf_op jit(solution)/shard_map/all_to_all | solution.py:13
Sparse Core Ops, SparseCore 0:
  32.5 44.9 all-reduce.2
